TPU v7x, 32 devices: a whole 2x2x4 slice. The times are simulated.
32 devices in a mesh: rep: 2 (over y), fsdp: 16 (over z, x, core).
Axes of the slice: x: 2, y: 2, z: 4, core: 2. Of those that a mesh axis runs over, the one named last changes fastest.
Arguments:
- tokens: bfloat16 [16384, 4096], P(('rep', 'fsdp')), may hold values from -6 to 6
- value_cot: bfloat16 [16384, 1024], P(('rep', 'fsdp')), may hold values from -6 to 6
- value_weight: bfloat16 [2, 4096, 1024], P('rep', 'fsdp'), may hold values from -0.09375 to 0.09375
- global_params: float32 [2097152], P('fsdp'), may hold values from -6 to 6
- local_params: float32 [2, 2097152], P('rep', 'fsdp'), may hold values from -6 to 6
- momentum: float32 [2097152], P('fsdp'), may hold values from -3 to 3
Outputs:
- token_grad: bfloat16 [16384, 4096], P(('rep', 'fsdp'))
- value_grad: float32 [2, 4096, 1024], P('rep', 'fsdp')
- new_global: float32 [2097152], P('fsdp')
- new_moment: float32 [2097152], P('fsdp')
All inputs are finite; a program needn't handle non-finite values.
Results may differ from a plain program's by a relative error of at most 0.001.
Values may be sent and summed in bfloat16 or wider, within the bound.
A program may use at most 128 MiB of HBM per device.

v0:
```python
import jax
import jax.numpy as jnp
from jax import lax
from jax.sharding import PartitionSpec as P


def grad_term(tokens, columns):
    return lax.dot_general(
        tokens, columns, (((0,), (0,)), ((), ())), preferred_element_type=jnp.float32
    )


def shards(tokens, value_cot, value_weight, global_params, local_params, momentum):
    weight = value_weight[0]
    token_grad = lax.dot_general(
        value_cot,
        lax.all_gather(weight, "fsdp", axis=0, tiled=True),
        (((1,), (1,)), ((), ())),
        preferred_element_type=jnp.float32,
    ).astype(jnp.bfloat16)
    groups = lax.axis_size("fsdp")
    factor = 1.0 / jnp.sqrt(jnp.float32(tokens.shape[0] * groups))
    summed = lax.psum_scatter(grad_term(tokens, value_cot), "fsdp", scatter_dimension=0, tiled=True)
    value_grad = (summed * factor)[None]
    totals = lax.psum(local_params[0], "rep")
    pseudo = global_params - totals / lax.axis_size("rep")
    new_moment = 0.9 * momentum + pseudo
    new_global = global_params - 0.7 * (pseudo + 0.9 * new_moment)
    return (token_grad, value_grad, new_global, new_moment)


def solution(mesh):
    in_specs = (
        P(("rep", "fsdp"), None),
        P(("rep", "fsdp"), None),
        P("rep", "fsdp", None),
        P("fsdp"),
        P("rep", "fsdp"),
        P("fsdp"),
    )
    out_specs = (P(("rep", "fsdp"), None), P("rep", "fsdp", None), P("fsdp"), P("fsdp"))
    return jax.shard_map(shards, mesh=mesh, in_specs=in_specs, out_specs=out_specs, check_vma=False)
```

profile of v0, /device:TPU:0, one launch (start us, length us, event | category | flops | bytes accessed | tf_op | source)
XLA Modules:
  0.0 277.8 jit_solution(12506146668002710478)
XLA Ops:
  8.0 0.0 copy-start
  8.0 0.0 all-reduce.2.cloned.1.call-start
  8.1 0.7 all-reduce.2.cloned.1.call-update
  8.7 0.0 all-gather.3.cloned.1.call-start
  8.8 0.5 all-gather.3.cloned.1.call-update
  9.3 0.0 reduce-scatter.2.cloned.1.call-start
  9.4 0.0 copy-done
  9.4 10.6 %fusion.5 = f32[4096,1024]{1,0:T(8,128)} fusion(bf16[512,4096]{1,0:T(8,128)(2,1)} %param.6, bf16[512,1024]{1,0:T(8,128)(2,1)S(1)} %copy-done), kind=kOutput, calls=%fused_computation.7 | convolution fusion | flops 4294967296 | bytes 22020096 | tf_op jit(solution)/shard_map/dot_general | solution.py:8
  20.0 0.0 copy-start.1
  20.0 0.0 copy-start.2
  20.0 0.0 reduce-scatter.2.cloned.1.call-update
  20.0 22.5 %all-reduce.2.cloned.1.call-done = f32[131072]{0:T(1024)} async-done(((f32[131072]{0:T(1024)}), f32[131072]{0:T(1024)}) %all-reduce.2.cloned.1.call-update) | async-done | bytes 524304 | tf_op jit(solution)/shard_map/psum | solution.py:25
  42.5 0.0 copy-done.1
  42.5 0.0 copy-done.2
  42.5 2.1 multiply_subtract_fusion
  44.7 43.5 %all-gather.3.cloned.1.call-done = bf16[1,4096,1024]{2,1,0:T(8,128)(2,1)} async-done(((bf16[1,256,1024]{2,1,0:T(8,128)(2,1)}), bf16[1,4096,1024]{2,1,0:T(8,128)(2,1)}) %all-gather.3.cloned.1.call-update) | async-done | bytes 8388624 | tf_op jit(solution)/shard_map/all_gather | solution.py:17
  88.2 9.5 %fusion.2 = bf16[512,4096]{1,0:T(8,128)(2,1)} fusion(bf16[512,1024]{1,0:T(8,128)(2,1)S(1)} %copy-done, bf16[1,4096,1024]{2,1,0:T(8,128)(2,1)} %all-gather.3.cloned.1.call-done), kind=kOutput, calls=%fused_computation.2 | convolution fusion | flops 4297064448 | bytes 13631488 | tf_op jit(solution)/shard_map/dot_general | solution.py:15
  97.7 170.4 %reduce-scatter.2.cloned.1.call-done = f32[256,1024]{1,0:T(8,128)} async-done(((f32[4096,1024]{1,0:T(8,128)}), f32[256,1024]{1,0:T(8,128)}) %reduce-scatter.2.cloned.1.call-update) | async-done | bytes 1048592 | tf_op jit(solution)/shard_map/reduce_scatter | solution.py:23
  268.0 2.3 multiply_bitcast_fusion
Async XLA Ops:
  8.0 1.4 copy-start
  8.0 34.5 %all-reduce.2.cloned.1.call-start = ((), (), s32[]{:S(2)}) async-start(), calls=%async_computation.2 | async-start | bytes 1048576 | tf_op jit(solution)/shard_map/psum | solution.py:25
  8.7 79.4 %all-gather.3.cloned.1.call-start = ((), (), s32[]{:S(2)}) async-start(), calls=%async_computation.3 | async-start | bytes 8912896 | tf_op jit(solution)/shard_map/all_gather | solution.py:17
  9.3 258.7 %reduce-scatter.2.cloned.1.call-start = ((), (), s32[]{:S(2)}) async-start(), calls=%async_computation.1 | async-start | bytes 17825792 | tf_op jit(solution)/shard_map/reduce_scatter | solution.py:23
  20.0 22.6 %copy-start.1 = (f32[131072]{0:T(1024)S(1)}, f32[131072]{0:T(1024)}, u32[]{:S(2)}) copy-start(f32[131072]{0:T(1024)} %param.9) | copy-start | bytes 1572868
  20.0 22.6 %copy-start.2 = (f32[131072]{0:T(1024)S(1)}, f32[131072]{0:T(1024)}, u32[]{:S(2)}) copy-start(f32[131072]{0:T(1024)} %param.11) | copy-start | bytes 1572868
Sparse Core Ops, SparseCore 0:
  11.1 31.3 all-reduce.1
Sparse Core Ops, SparseCore 1:
  11.4 76.7 all-gather.2
  92.2 175.8 reduce-scatter.1
where the time goes:
time: 278 us
  waiting for transfers between devices  238 us (86%)
  matrix products  20 us (7%)
  between operations  15.5 us (6%)
  other arithmetic  4.49 us (2%)
    reduce_scatter x1, waiting for transfers between devices, shards(): lax.psum_scatter(grad_term(tokens, value_cot), 'fsdp', scatter_dimension=...  170 us
    all_gather x1, waiting for transfers between devices, shards(): lax.all_gather(weight, 'fsdp', axis=0, tiled=True)  43.5 us
    psum x1, waiting for transfers between devices, shards(): totals = lax.psum(local_params[0], 'rep')  22.5 us
    dot_general x1, matrix products, grad_term(): lax.dot_general(tokens, columns, (((0,), (0,)), ((), ())), preferred_elem...  10.6 us
    dot_general x1, matrix products, shards(): lax.dot_general(value_cot, lax.all_gather(weight, 'fsdp', axis=0, tiled=T...  9.45 us
  transfers between devices with their start and end apart: 3, of which 3 were waited for; matrix products, arithmetic and copies ran while one was open for 8% of the time, Pallas kernels for 0%

commit v1 on v0

--- a/solution.py
+++ b/solution.py
@@ -22,7 +22,9 @@
     factor = 1.0 / jnp.sqrt(jnp.float32(tokens.shape[0] * groups))
     summed = lax.psum_scatter(grad_term(tokens, value_cot), "fsdp", scatter_dimension=0, tiled=True)
     value_grad = (summed * factor)[None]
-    totals = lax.psum(local_params[0], "rep")
+    x = local_params[0]
+    parts = lax.all_gather(x, "rep")
+    totals = jnp.sum(parts, axis=0)
     pseudo = global_params - totals / lax.axis_size("rep")
     new_moment = 0.9 * momentum + pseudo
     new_global = global_params - 0.7 * (pseudo + 0.9 * new_moment)

time: 278 us -> 299 us (1.076)
  waiting for transfers between devices: 238 us -> 259 us
    all_gather x1, waiting for transfers between devices: 43.5 us -> 72.6 us  [shards(): lax.all_gather(weight, 'fsdp', axis=0, tiled=True)]
    psum x1 -> x0, waiting for transfers between devices: 22.5 us -> none  [shards(): totals = lax.psum(local_params[0], 'rep')]
    all_gather x0 -> x1, waiting for transfers between devices: none -> 14.2 us  [shards(): parts = lax.all_gather(x, 'rep')]
where the time goes in v1:
time: 299 us
  waiting for transfers between devices  259 us (87%)
  matrix products  20.1 us (7%)
  between operations  13.8 us (5%)
  other arithmetic  6.19 us (2%)
    reduce_scatter x1, waiting for transfers between devices, shards(): lax.psum_scatter(grad_term(tokens, value_cot), 'fsdp', scatter_dimension=...  171 us
    all_gather x1, waiting for transfers between devices, shards(): lax.all_gather(weight, 'fsdp', axis=0, tiled=True)  72.6 us
    all_gather x1, waiting for transfers between devices, shards(): parts = lax.all_gather(x, 'rep')  14.2 us
    dot_general x1, matrix products, grad_term(): lax.dot_general(tokens, columns, (((0,), (0,)), ((), ())), preferred_elem...  10.6 us
    dot_general x1, matrix products, shards(): lax.dot_general(value_cot, lax.all_gather(weight, 'fsdp', axis=0, tiled=T...  9.45 us
  transfers between devices with their start and end apart: 3, of which 3 were waited for; matrix products, arithmetic and copies ran while one was open for 8% of the time, Pallas kernels for 0%

profile of v1, /device:TPU:0, one launch (start us, length us, event | category | flops | bytes accessed | tf_op | source)
XLA Modules:
  0.0 299.0 jit_solution(2547519507922141982)
XLA Ops:
  7.2 0.0 copy-start
  7.2 0.0 all-gather.7.cloned.1.call-start
  7.2 0.7 all-gather.7.cloned.1.call-update
  7.9 0.0 all-gather.5.cloned.1.call-start
  8.0 0.7 all-gather.5.cloned.1.call-update
  8.7 0.0 reduce-scatter.2.cloned.1.call-start
  8.7 0.0 copy-done
  8.7 10.6 %fusion.5 = f32[4096,1024]{1,0:T(8,128)} fusion(bf16[512,4096]{1,0:T(8,128)(2,1)} %param.6, bf16[512,1024]{1,0:T(8,128)(2,1)S(1)} %copy-done), kind=kOutput, calls=%fused_computation.7 | convolution fusion | flops 4294967296 | bytes 22020096 | tf_op jit(solution)/shard_map/dot_general | solution.py:8
  19.4 0.0 copy-start.1
  19.4 0.0 copy-start.2
  19.4 0.0 reduce-scatter.2.cloned.1.call-update
  19.4 14.2 %all-gather.7.cloned.1.call-done = f32[2,1,131072]{2,1,0:T(1,128)} async-done(((f32[1,1,131072]{2,1,0:T(1,128)}), f32[2,1,131072]{2,1,0:T(1,128)}) %all-gather.7.cloned.1.call-update) | async-done | bytes 1048592 | tf_op jit(solution)/shard_map/all_gather | solution.py:26
  33.6 2.7 reduce_sum.9
  36.3 0.0 copy-done.1
  36.3 0.0 copy-done.2
  36.3 1.1 multiply_subtract_fusion
  37.4 72.6 %all-gather.5.cloned.1.call-done = bf16[1,4096,1024]{2,1,0:T(8,128)(2,1)} async-done(((bf16[1,256,1024]{2,1,0:T(8,128)(2,1)}), bf16[1,4096,1024]{2,1,0:T(8,128)(2,1)}) %all-gather.5.cloned.1.call-update) | async-done | bytes 8388624 | tf_op jit(solution)/shard_map/all_gather | solution.py:17
  110.1 9.5 %fusion.2 = bf16[512,4096]{1,0:T(8,128)(2,1)} fusion(bf16[512,1024]{1,0:T(8,128)(2,1)S(1)} %copy-done, bf16[1,4096,1024]{2,1,0:T(8,128)(2,1)} %all-gather.5.cloned.1.call-done), kind=kOutput, calls=%fused_computation.2 | convolution fusion | flops 4297064448 | bytes 13631488 | tf_op jit(solution)/shard_map/dot_general | solution.py:15
  119.5 170.6 %reduce-scatter.2.cloned.1.call-done = f32[256,1024]{1,0:T(8,128)} async-done(((f32[4096,1024]{1,0:T(8,128)}), f32[256,1024]{1,0:T(8,128)}) %reduce-scatter.2.cloned.1.call-update) | async-done | bytes 1048592 | tf_op jit(solution)/shard_map/reduce_scatter | solution.py:23
  290.1 2.3 multiply_bitcast_fusion
Async XLA Ops:
  7.2 1.5 copy-start
  7.2 26.4 %all-gather.7.cloned.1.call-start = ((), (), s32[]{:S(2)}) async-start(), calls=%async_computation.3 | async-start | bytes 1572864 | tf_op jit(solution)/shard_map/all_gather | solution.py:26
  7.9 102.1 %all-gather.5.cloned.1.call-start = ((), (), s32[]{:S(2)}) async-start(), calls=%async_computation.2 | async-start | bytes 8912896 | tf_op jit(solution)/shard_map/all_gather | solution.py:17
  8.7 281.4 %reduce-scatter.2.cloned.1.call-start = ((), (), s32[]{:S(2)}) async-start(), calls=%async_computation.1 | async-start | bytes 17825792 | tf_op jit(solution)/shard_map/reduce_scatter | solution.py:23
  19.4 17.0 %copy-start.1 = (f32[131072]{0:T(1024)S(1)}, f32[131072]{0:T(1024)}, u32[]{:S(2)}) copy-start(f32[131072]{0:T(1024)} %param.9) | copy-start | bytes 1572868
  19.4 17.0 %copy-start.2 = (f32[131072]{0:T(1024)S(1)}, f32[131072]{0:T(1024)}, u32[]{:S(2)}) copy-start(f32[131072]{0:T(1024)} %param.11) | copy-start | bytes 1572868
Sparse Core Ops, SparseCore 0:
  9.5 23.9 all-gather.6
  35.7 74.2 all-gather.4
  114.2 175.8 reduce-scatter.1
